TPU v7x, 512 devices: a whole 4x8x8 slice. The times are simulated.
512 devices in a mesh: row: 16 (over y, core), col: 32 (over x, z).
Axes of the slice: x: 4, y: 8, z: 8, core: 2. Of those that a mesh axis runs over, the one named last changes fastest.
Arguments:
- lhat: float32 [4096, 256, 256], P(('row', 'col')), may hold values from -0.375 to 0.375
- ainv_anc: float32 [4096, 256, 256], P(('row', 'col')), may hold values from -1.25 to 1.25
- diag_inv: float32 [32, 256, 256], P('col', 'row'), may hold values from -0.6 to 2, as said below
- targets: int32 [4096, 1], P(('row', 'col')), may hold values from 0 to 31
Outputs:
- diag_blocks: float32 [32, 256, 256], P('col', 'row')
Inputs may be any that keep to these rules, and one draw needn't show every extreme that they name: `diag_inv`: each block is lower triangular with its diagonal entries between 0.5 and 2.
All inputs are finite; a program needn't handle non-finite values.
Results may differ from a plain program's by a relative error of at most 0.0003.
Values sent between devices are 32-bit elements; how exact they have to be, the bound alone decides.
A program may use at most 64 MiB of HBM per device.

v0:
```python
import jax
import jax.numpy as jnp
from jax import lax
from jax.sharding import PartitionSpec as P


def laid_out(tiles, dim):
    lengths = list(tiles.shape[1:])
    lengths[dim] *= tiles.shape[0]
    return jnp.moveaxis(tiles, 0, dim).reshape(lengths)


def copy_for_each(x, axis):
    length = lax.axis_size(axis)
    return lax.all_to_all(jnp.broadcast_to(x[None], (length, *x.shape)), axis, 0, 0, tiled=True)


def collect(x, axis, dim):
    return laid_out(copy_for_each(x, axis), dim)


def in_blocks(x, dim, length):
    lengths = x.shape
    tiles = x.reshape(*lengths[:dim], length, lengths[dim] // length, *lengths[dim + 1 :])
    return jnp.moveaxis(tiles, dim, 0)


def summed_on_arrival(x, axis, dim):
    length = lax.axis_size(axis)
    tiles = lax.all_to_all(in_blocks(x, dim, length), axis, 0, 0, tiled=True)
    return jnp.sum(tiles, axis=0)


def on_device(lhat, ainv_anc, diag_inv, targets):
    row_count = lax.axis_size("row")
    row_index = lax.axis_index("row")
    width = diag_inv.shape[2]
    row_share = width // row_count
    owned_count = diag_inv.shape[0]
    super_count = owned_count * lax.axis_size("col")
    col_start = row_index * row_share
    products = -jnp.einsum("shi,shj->sij", lhat, ainv_anc, precision=lax.Precision.HIGHEST)
    slot_ids = targets[:, 0]
    factor_piece = collect(diag_inv, "row", 1)
    col_slice = lax.dynamic_slice_in_dim(factor_piece, col_start, row_share, 2)
    gram_rows = jnp.einsum("kia,kib->kab", col_slice, factor_piece, precision=lax.Precision.HIGHEST)
    received = lax.all_to_all(products, "row", split_axis=1, concat_axis=0, tiled=True)
    ids_all = collect(slot_ids, "row", 0)
    labels = jnp.arange(super_count, dtype=jnp.int32)
    one_hot = (labels[:, None] == ids_all[None, :]).astype(jnp.float32)
    summed = jnp.einsum("kn,nij->kij", one_hot, received, precision=lax.Precision.HIGHEST)
    own_blocks = summed_on_arrival(summed, "col", 0)
    return own_blocks + gram_rows


def solution(mesh):
    placed = (
        P(("row", "col"), None, None),
        P(("row", "col"), None, None),
        P("col", "row", None),
        P(("row", "col"), None),
    )
    return jax.shard_map(
        on_device, mesh=mesh, in_specs=placed, out_specs=P("col", "row", None), check_vma=False
    )
```

profile of v0, /device:TPU:1, one launch (start us, length us, event | category | flops | bytes accessed | tf_op | source)
XLA Modules:
  0.0 125.0 jit_solution(12775095045599749959)
XLA Ops:
  0.0 0.0 copy-start
  0.0 1.4 %broadcast_in_dim.17 = s32[16,1,8]{2,1,0:T(1,128)} broadcast(s32[8]{0:T(128)} %bitcast.28), dimensions={2} | broadcast | bytes 544 | tf_op jit(solution)/shard_map/broadcast_in_dim | solution.py:15
  1.4 10.1 %all-to-all-start = ((s32[16,1,8]{2,1,0:T(1,128)}), s32[16,1,8]{2,1,0:T(1,128)S(1)}, u32[]{:S(2)}, u32[]{:S(2)}) async-start(s32[16,1,8]{2,1,0:T(1,128)} %broadcast_in_dim.17), calls=%async_computation | async-start | bytes 16384 | tf_op jit(solution)/shard_map/all_to_all | solution.py:15
  11.5 0.0 copy-done
  11.5 5.1 %convolution_negate_fusion = f32[8,256,256]{2,1,0:T(8,128)S(1)} fusion(f32[8,256,256]{2,1,0:T(8,128)S(1)} %copy-done, f32[8,256,256]{2,1,0:T(8,128)} %param.5), kind=kOutput, calls=%fused_computation.3 | convolution fusion | flops 1611137024 | bytes 6291456 | tf_op jit(solution)/shard_map/shi,shj->sij/dot_general | solution.py:42
  16.6 2.5 %copy.10 = f32[8,256,256]{2,0,1:T(8,128)} copy(f32[8,256,256]{2,1,0:T(8,128)S(1)} %convolution_negate_fusion) | data formatting | bytes 4194304 | tf_op jit(solution)/shard_map/neg | solution.py:42
  19.2 0.0 all-to-all-done
  19.2 7.3 %all-to-all-start.1 = ((f32[8,256,256]{2,0,1:T(8,128)}), f32[8,256,256]{2,0,1:T(8,128)}, u32[]{:S(2)}, u32[]{:S(2)}) async-start(f32[8,256,256]{2,0,1:T(8,128)} %copy.10), calls=%async_computation.1 | async-start | bytes 4194304 | tf_op jit(solution)/shard_map/all_to_all | solution.py:47
  26.4 0.5 broadcast.7
  26.9 0.7 reduce.4
  27.6 0.1 eq.16
  27.7 47.9 %all-to-all-done.1 = f32[8,256,256]{2,0,1:T(8,128)} async-done(((f32[8,256,256]{2,0,1:T(8,128)}), f32[8,256,256]{2,0,1:T(8,128)}, u32[]{:S(2)}, u32[]{:S(2)}) %all-to-all-start.1) | async-done | bytes 2097184 | tf_op jit(solution)/shard_map/all_to_all | solution.py:47
  75.6 0.0 copy-start.1
  75.6 2.4 %fusion.3 = f32[32,1,16,256]{3,0,2,1:T(8,128)S(1)} fusion(f32[8,16,16,256]{3,0,2,1:T(8,128)} %bitcast.2, s32[128]{0:T(128)S(1)} %eq.16), kind=kOutput, calls=%fused_computation.4 | convolution fusion | flops 201330688 | bytes 2621952 | tf_op jit(solution)/shard_map/kn,nij->kij/dot_general | solution.py:51
  78.0 0.3 copy.12
  78.4 25.2 %all_to_all.34 = f32[32,1,16,256]{3,2,1,0:T(8,128)S(1)} all-to-all(f32[32,1,16,256]{3,2,1,0:T(8,128)S(1)} %copy.12), channel_id=1, replica_groups=mesh['row'=16,'col'=32] {'col'}, dimensions={0} | all-to-all | bytes 1048576 | tf_op jit(solution)/shard_map/all_to_all | solution.py:30
  103.5 0.0 copy-done.1
  103.5 0.7 broadcast_in_dim.19
  104.3 8.1 %all-to-all-start.3 = ((f32[16,1,16,256]{3,2,1,0:T(8,128)}), f32[16,1,16,256]{3,2,1,0:T(8,128)S(1)}, u32[]{:S(2)}, u32[]{:S(2)}) async-start(f32[16,1,16,256]{3,2,1,0:T(8,128)} %broadcast_in_dim.19), calls=%async_computation.3 | async-start | bytes 524288 | tf_op jit(solution)/shard_map/all_to_all | solution.py:15
  112.4 11.5 %all-to-all-done.3 = f32[16,1,16,256]{3,2,1,0:T(8,128)S(1)} async-done(((f32[16,1,16,256]{3,2,1,0:T(8,128)}), f32[16,1,16,256]{3,2,1,0:T(8,128)S(1)}, u32[]{:S(2)}, u32[]{:S(2)}) %all-to-all-start.3) | async-done | bytes 262176 | tf_op jit(solution)/shard_map/all_to_all | solution.py:15
  123.9 1.0 fusion.6
  (1 shorter events, 0.0 us)
Async XLA Ops:
  0.0 11.5 %copy-start = (f32[8,256,256]{2,1,0:T(8,128)S(1)}, f32[8,256,256]{2,1,0:T(8,128)}, u32[]{:S(2)}) copy-start(f32[8,256,256]{2,1,0:T(8,128)} %param.4) | copy-start | bytes 6291460
  1.4 17.7 %all-to-all-start = ((s32[16,1,8]{2,1,0:T(1,128)}), s32[16,1,8]{2,1,0:T(1,128)S(1)}, u32[]{:S(2)}, u32[]{:S(2)}) async-start(s32[16,1,8]{2,1,0:T(1,128)} %broadcast_in_dim.17), calls=%async_computation | async-start | bytes 16384 | tf_op jit(solution)/shard_map/all_to_all | solution.py:15
  19.2 56.4 %all-to-all-start.1 = ((f32[8,256,256]{2,0,1:T(8,128)}), f32[8,256,256]{2,0,1:T(8,128)}, u32[]{:S(2)}, u32[]{:S(2)}) async-start(f32[8,256,256]{2,0,1:T(8,128)} %copy.10), calls=%async_computation.1 | async-start | bytes 4194304 | tf_op jit(solution)/shard_map/all_to_all | solution.py:47
  75.6 28.0 %copy-start.1 = (f32[1,16,256]{2,1,0:T(8,128)S(1)}, f32[1,16,256]{2,1,0:T(8,128)}, u32[]{:S(2)}) copy-start(f32[1,16,256]{2,1,0:T(8,128)} %param.6) | copy-start | bytes 49156
  104.3 19.7 %all-to-all-start.3 = ((f32[16,1,16,256]{3,2,1,0:T(8,128)}), f32[16,1,16,256]{3,2,1,0:T(8,128)S(1)}, u32[]{:S(2)}, u32[]{:S(2)}) async-start(f32[16,1,16,256]{3,2,1,0:T(8,128)} %broadcast_in_dim.19), calls=%async_computation.3 | async-start | bytes 524288 | tf_op jit(solution)/shard_map/all_to_all | solution.py:15
where the time goes:
time: 125 us
  waiting for transfers between devices  59.4 us (48%)
  starting transfers between devices  25.5 us (20%)
  blocking collectives  25.2 us (20%)
  matrix products  8.59 us (7%)
  local copies, waits for them, and re-layouts  5.56 us (4%)
    all_to_all x1, waiting for transfers between devices, on_device(): lax.all_to_all(products, 'row', split_axis=1, concat_axis=0, tiled=True)  47.9 us
    all_to_all x1, blocking collectives, summed_on_arrival(): tiles = lax.all_to_all(in_blocks(x, dim, length), axis, 0, 0, tiled=True)  25.2 us
    all_to_all x2, starting transfers between devices, copy_for_each(): lax.all_to_all(jnp.broadcast_to(x[None], (length, *x.shape)), axis, 0, 0,...  18.2 us
    all_to_all x2, waiting for transfers between devices, copy_for_each(): lax.all_to_all(jnp.broadcast_to(x[None], (length, *x.shape)), axis, 0, 0,...  11.5 us
    all_to_all x1, starting transfers between devices, on_device(): lax.all_to_all(products, 'row', split_axis=1, concat_axis=0, tiled=True)  7.27 us
    dot_general x1, matrix products, on_device(): jnp.einsum('shi,shj->sij', lhat, ainv_anc, precision=lax.Precision.HIGHEST)  5.11 us
    neg x1, local copies, waits for them, and re-layouts, on_device(): -jnp.einsum('shi,shj->sij', lhat, ainv_anc, precision=lax.Precision.HIGHEST)  2.52 us
  transfers between devices with their start and end apart: 3, of which 2 were waited for; matrix products, arithmetic and copies ran while one was open for 7% of the time, Pallas kernels for 0%

commit v1 on v0

v1 whole, which is shorter than its diff:
```python
import functools

import jax
import jax.numpy as jnp
from jax import lax
from jax.experimental import pallas as pl
from jax.experimental.pallas import tpu as pltpu
from jax.sharding import PartitionSpec as P

MESH = pl.DeviceIdType.MESH
LANES = 128
ROWS = 16


def split(x):
    hi = x.astype(jnp.bfloat16)
    lo = (x - hi.astype(jnp.float32)).astype(jnp.bfloat16)
    return hi, lo


def transposed_product(a, b):
    ah, al = split(a)
    bh, bl = split(b)
    left = jnp.concatenate([ah, ah, al], axis=0)
    right = jnp.concatenate([bh, bl, bh], axis=0)
    return lax.dot_general(left, right, (((0,), (0,)), ((), ())), preferred_element_type=jnp.float32)


def kernel(
    dims, slots,
    lhat, ainv, dinv, targets, out,
    left, right, fac, ids, prod, rx, last_a, last_b,
    st_y, st_z, rc_y, rc_z, fin_y, fin_z, r2_y, r2_z,
    in_sem, x_send, x_recv, t_send, t_recv,
    ys, yr, zs, zr, y2s, y2r, z2s, z2r,
):
    nx, ny, nz = dims
    row, col = lax.axis_index("row"), lax.axis_index("col")
    y, c = row // 2, row % 2
    x, z = col // nz, col % nz
    none = slots + 1
    half_k = nx * nz // 2
    half_x = nx // 2

    def at(xx, yy, zz, cc):
        return (yy * 2 + cc, xx * nz + zz)

    partner = at(x, y, z, 1 - c)

    def loads(s):
        return (
            pltpu.make_async_copy(lhat.at[s], left.at[s], in_sem.at[0, s]),
            pltpu.make_async_copy(ainv.at[s], right.at[s], in_sem.at[1, s]),
        )

    fac_load = pltpu.make_async_copy(dinv.at[0], fac, in_sem.at[0, slots])
    ids_load = pltpu.make_async_copy(targets, ids, in_sem.at[1, slots])
    fac_load.start()
    ids_load.start()
    for s in range(slots):
        for load in loads(s):
            load.start()

    barrier = pltpu.get_barrier_semaphore()
    peers = [partner]
    for step in (1, ny - 1):
        peers.append(at(x, (y + step) % ny, z, c))
    for step in (1, nz - 1):
        peers.append(at(x, y, (z + step) % nz, c))
    for step in range(1, nx):
        peers.append(at((x + step) % nx, y, z, c))
    for peer in peers:
        pl.semaphore_signal(barrier, inc=1, device_id=peer, device_id_type=MESH)

    prod[none] = jnp.zeros(prod.shape[1:], jnp.float32)
    rx[none] = jnp.zeros(rx.shape[1:], jnp.float32)
    fac_load.wait()
    gram = transposed_product(fac[...], fac[...])
    prod[0] = gram.reshape(prod.shape[1:])
    ids_load.wait()
    pl.semaphore_wait(barrier, len(peers))

    def table(k, carry):
        found = jnp.where(col == k, 0, none)
        for s in range(slots):
            found = jnp.where(ids[s] == k, s + 1, found)
        last_a[k] = found
        return carry

    lax.fori_loop(0, nx * nz, table, 0)
    table_copy = pltpu.make_async_remote_copy(
        last_a, last_b, t_send, t_recv, device_id=partner, device_id_type=MESH
    )
    table_copy.start()

    exchanges = []

    def exchange(s):
        copy = pltpu.make_async_remote_copy(
            prod.at[s, :, 1 - c], rx.at[s], x_send.at[s], x_recv.at[s],
            device_id=partner, device_id_type=MESH,
        )
        copy.start()
        exchanges.append(copy)

    for s in range(slots):
        for load in loads(s):
            load.wait()
        value = transposed_product(left[s], right[s])
        before = jnp.where(ids[s] == col, 0, none)
        for e in range(s):
            before = jnp.where(ids[e] == ids[s], e + 1, before)
        prod[s + 1] = prod[before] - value.reshape(prod.shape[1:])
        exchange(s)
    exchange(slots)
    table_copy.wait()
    for copy in exchanges:
        copy.wait()

    def local_y(k, yb):
        return prod[last_a[k], yb, c, :, 0:LANES] + rx[last_b[k], yb, :, 0:LANES]

    def local_z(k):
        return prod[last_a[k], :, c, :, LANES:] + rx[last_b[k], :, :, LANES:]

    unroll = 4 if half_k % 4 == 0 else 1

    def over_k(body):
        def some(i, carry):
            for j in range(unroll):
                body(i * unroll + j)
            return carry

        lax.fori_loop(0, half_k // unroll, some, 0)

    sends = []

    def hop(axis, way, half, h):
        n = ny if axis == "y" else nz
        long = half == way
        hops = n // 2 if long else n // 2 - 1
        if h >= hops:
            return
        sign = 1 if way == 0 else -1
        first = 0 if long else n // 2
        rc, st, ss, rs = (rc_y, st_y, ys, yr) if axis == "y" else (rc_z, st_z, zs, zr)
        here = y if axis == "y" else z
        dest = (here + sign * (hops - h) + n) % n
        peer = (here + sign + n) % n
        device = at(x, peer, z, c) if axis == "y" else at(x, y, peer, c)
        if h == 0:
            src = st.at[way, half]
        else:
            src = rc.at[way, first + h - 1]
            pltpu.make_async_remote_copy(
                src, src, ss.at[way, first + h - 1], rs.at[way, first + h - 1],
                device_id=device, device_id_type=MESH,
            ).wait_recv()
        if axis == "y":
            def body(k):
                v = local_y(half * half_k + k, dest)
                src[k] = v if h == 0 else src[k] + v

            over_k(body)
        else:
            for i in range(half_x):
                v = local_z((half * half_x + i) * nz + dest)
                src[i] = v if h == 0 else src[i] + v
        copy = pltpu.make_async_remote_copy(
            src, rc.at[way, first + h], ss.at[way, first + h], rs.at[way, first + h],
            device_id=device, device_id_type=MESH,
        )
        copy.start()
        sends.append(copy)

    for h in range(max(ny, nz) // 2):
        for part in (0, 1):
            for axis in ("y", "z"):
                for way in (0, 1):
                    hop(axis, way, way if part == 0 else 1 - way, h)

    def arrived(axis, way, half):
        n = ny if axis == "y" else nz
        long = half == way
        hops = n // 2 if long else n // 2 - 1
        if hops == 0:
            return None
        m = (0 if long else n // 2) + hops - 1
        rc, ss, rs = (rc_y, ys, yr) if axis == "y" else (rc_z, zs, zr)
        pltpu.make_async_remote_copy(
            rc.at[way, m], rc.at[way, m], ss.at[way, m], rs.at[way, m],
            device_id=partner, device_id_type=MESH,
        ).wait_recv()
        return rc.at[way, m]

    for half in (0, 1):
        got_y = [g for g in (arrived("y", way, half) for way in (0, 1)) if g is not None]
        got_z = [g for g in (arrived("z", way, half) for way in (0, 1)) if g is not None]

        def total_y(k):
            v = local_y(half * half_k + k, y)
            for g in got_y:
                v = v + g[k]
            fin_y[half * half_k + k] = v

        over_k(total_y)
        for i in range(half_x):
            xi = half * half_x + i
            v = local_z(xi * nz + z)
            for g in got_z:
                v = v + g[i]
            fin_z[pl.ds(xi * ny, ny)] = v

    n_y, n_z = nx * nz, nx * ny
    place = x * ny + y

    def send_y(d):
        to = (col + d) % n_y
        return pltpu.make_async_remote_copy(
            fin_y.at[to], r2_y.at[col], y2s.at[d], y2r.at[col],
            device_id=(row, to), device_id_type=MESH,
        )

    def send_z(d):
        to = (place + d) % n_z
        return pltpu.make_async_remote_copy(
            fin_z.at[to], r2_z.at[place], z2s.at[d], z2r.at[place],
            device_id=at(to // ny, to % ny, z, c), device_id_type=MESH,
        )

    def start_y(d, carry):
        send_y(d).start()
        return carry

    def start_z(d, carry):
        send_z(d).start()
        return carry

    lax.fori_loop(1, n_y, start_y, 0)
    lax.fori_loop(1, n_z, start_z, 0)

    def take_y(d, total):
        src = (col + d) % n_y
        pltpu.make_async_remote_copy(
            r2_y.at[src], r2_y.at[src], y2s.at[d], y2r.at[src],
            device_id=partner, device_id_type=MESH,
        ).wait_recv()
        return total + r2_y[src]

    def take_z(d, total):
        src = (place + d) % n_z
        pltpu.make_async_remote_copy(
            r2_z.at[src], r2_z.at[src], z2s.at[d], z2r.at[src],
            device_id=partner, device_id_type=MESH,
        ).wait_recv()
        return total + r2_z[src]

    out[0, :, 0:LANES] = lax.fori_loop(1, n_y, take_y, fin_y[col])
    out[0, :, LANES:] = lax.fori_loop(1, n_z, take_z, fin_z[place])

    for copy in sends:
        copy.wait_send()

    def done_y(d, carry):
        send_y(d).wait_send()
        return carry

    def done_z(d, carry):
        send_z(d).wait_send()
        return carry

    lax.fori_loop(1, n_y, done_y, 0)
    lax.fori_loop(1, n_z, done_z, 0)


def on_device(dims, lhat, ainv_anc, diag_inv, targets):
    nx, ny, nz = dims
    slots, height, width = lhat.shape
    f32 = jnp.float32
    vm = pltpu.VMEM
    dma = pltpu.SemaphoreType.DMA
    k_all, half_k, half_x = nx * nz, nx * nz // 2, nx // 2
    scratch = [
        vm((slots, height, width), f32),
        vm((slots, height, width), f32),
        vm((ROWS, width), f32),
        pltpu.SMEM((slots,), jnp.int32),
        vm((slots + 2, ny, 2, ROWS, width), f32),
        vm((slots + 2, ny, ROWS, width), f32),
        pltpu.SMEM((k_all,), jnp.int32),
        pltpu.SMEM((k_all,), jnp.int32),
        vm((2, 2, half_k, ROWS, LANES), f32),
        vm((2, 2, half_x, ny, ROWS, LANES), f32),
        vm((2, ny - 1, half_k, ROWS, LANES), f32),
        vm((2, nz - 1, half_x, ny, ROWS, LANES), f32),
        vm((k_all, ROWS, LANES), f32),
        vm((nx * ny, ROWS, LANES), f32),
        vm((k_all, ROWS, LANES), f32),
        vm((nx * ny, ROWS, LANES), f32),
        dma((2, slots + 1)),
        dma((slots + 1,)),
        dma((slots + 1,)),
        dma,
        dma,
        dma((2, ny - 1)),
        dma((2, ny - 1)),
        dma((2, nz - 1)),
        dma((2, nz - 1)),
        dma((k_all,)),
        dma((k_all,)),
        dma((nx * ny,)),
        dma((nx * ny,)),
    ]
    return pl.pallas_call(
        functools.partial(kernel, dims, slots),
        out_shape=jax.ShapeDtypeStruct(diag_inv.shape, f32),
        in_specs=[pl.BlockSpec(memory_space=pl.ANY)] * 4,
        out_specs=pl.BlockSpec(memory_space=vm),
        scratch_shapes=scratch,
        compiler_params=pltpu.CompilerParams(
            collective_id=0, has_side_effects=True
        ),
        name="selected_blocks",
    )(lhat, ainv_anc, diag_inv, targets.reshape(slots))


def solution(mesh, nz=8):
    dims = (mesh.shape["col"] // nz, mesh.shape["row"] // 2, nz)
    placed = (
        P(("row", "col"), None, None),
        P(("row", "col"), None, None),
        P("col", "row", None),
        P(("row", "col"), None),
    )
    return jax.shard_map(
        functools.partial(on_device, dims), mesh=mesh, in_specs=placed, out_specs=P("col", "row", None), check_vma=False
    )
```

time: 125 us -> 56.4 us (0.45)
  waiting for transfers between devices: 59.4 us -> 0 us
  Pallas kernels: 0 us -> 54.7 us
  starting transfers between devices: 25.5 us -> 0 us
  blocking collectives: 25.2 us -> 0 us
  matrix products: 8.59 us -> 0 us
  local copies, waits for them, and re-layouts: 5.56 us -> 1.32 us
    all_to_all x3 -> x0, waiting for transfers between devices: 59.4 us -> none  [the longest x1 47.9 us: on_device(): lax.all_to_all(products, 'row', split_axis=1, concat_axis=0, tiled=True)]
    pallas_call x0 -> x1, Pallas kernels: none -> 54.7 us  [on_device(): pl.pallas_call(functools.partial(kernel, dims, slots), out_shape=jax.Shap...]
    all_to_all x3 -> x0, starting transfers between devices: 25.5 us -> none  [the longest x2 18.2 us: copy_for_each(): lax.all_to_all(jnp.broadcast_to(x[None], (length, *x.shape)), axis, 0, 0,...]
    all_to_all x1 -> x0, blocking collectives: 25.2 us -> none  [summed_on_arrival(): tiles = lax.all_to_all(in_blocks(x, dim, length), axis, 0, 0, tiled=True)]
    dot_general x3 -> x0, matrix products: 8.59 us -> none  [the longest x1 5.11 us: on_device(): jnp.einsum('shi,shj->sij', lhat, ainv_anc, precision=lax.Precision.HIGHEST)]
    neg x1 -> x0, local copies, waits for them, and re-layouts: 2.52 us -> none  [on_device(): -jnp.einsum('shi,shj->sij', lhat, ainv_anc, precision=lax.Precision.HIGHEST)]
    broadcast_in_dim x2 -> x0, local copies, waits for them, and re-layouts: 2.12 us -> none  [copy_for_each(): jnp.broadcast_to(x[None], (length, *x.shape))]
    unnamed x4 -> x1, local copies, waits for them, and re-layouts: 0.01 us -> 1.32 us
  transfers between devices with their start and end apart: 3 -> 0, of which waited for: 2 -> 0; matrix products, arithmetic and copies ran while one was open for 7% -> 0% of each run, Pallas kernels for 0% -> 0%
where the time goes in v1:
time: 56.4 us; the launch traced here: 56.1 us
  Pallas kernels  54.7 us (97%)
  local copies, waits for them, and re-layouts  1.32 us (2%)
    pallas_call x1, Pallas kernels, on_device(): pl.pallas_call(functools.partial(kernel, dims, slots), out_shape=jax.Shap...  54.7 us
    unnamed x1, local copies, waits for them, and re-layouts  1.32 us

profile of v1, /device:TPU:1, one launch (start us, length us, event | category | flops | bytes accessed | tf_op | source)
XLA Modules:
  0.0 56.1 jit_solution(10916102176826717881)
XLA Ops:
  0.0 54.7 %selected_blocks.1 = f32[1,16,256]{2,1,0:T(8,128)} custom-call(f32[8,256,256]{2,1,0:T(8,128)} %lhat.1, f32[8,256,256]{2,1,0:T(8,128)} %ainv.1, f32[1,16,256]{2,1,0:T(8,128)} %dinv.1, s32[8]{0:T(128)} %bitcast.1), custom_call_target="tpu_custom_call" | custom-call | tf_op jit(solution)/shard_map/selected_blocks/pallas_call | solution.py:314
  54.7 1.3 %copy.6 = f32[1,16,256]{2,1,0:T(8,128)} copy(f32[1,16,256]{2,1,0:T(8,128)} %selected_blocks.1) | data formatting | bytes 32768

commit v2 on v0

v2 whole, which is shorter than its diff:
```python
import functools

import jax
import jax.numpy as jnp
from jax import lax
from jax.experimental import pallas as pl
from jax.experimental.pallas import tpu as pltpu
from jax.sharding import PartitionSpec as P

MESH = pl.DeviceIdType.MESH
LANES = 128
SUB = 8


def split(x):
    hi = x.astype(jnp.bfloat16)
    lo = (x - hi.astype(jnp.float32)).astype(jnp.bfloat16)
    return hi, lo


def transposed_product(a, b):
    ah, al = split(a)
    bh, bl = split(b)
    left = jnp.concatenate([ah, ah, al], axis=0)
    right = jnp.concatenate([bh, bl, bh], axis=0)
    return lax.dot_general(left, right, (((0,), (0,)), ((), ())), preferred_element_type=jnp.float32)


def kernel(
    dims, slots,
    lhat, ainv, dinv, targets, out,
    both, fac, ids, prod, rx_u, rx_d, rx_p, last_a, last_o,
    st_uy, st_uz, st_py, st_pz, rc_uy, rc_uz, rc_py, rc_pz,
    fin_uy, fin_uz, fin_py, fin_pz, r2_uy, r2_uz, r2_py, r2_pz,
    in_sem, xu_s, xu_r, xd_s, xd_r, xp_s, xp_r, t_s, t_r,
    uys, uyr, uzs, uzr, ps, pr,
    fus, fuyr, fuzr, fps, fpyr, fpzr,
):
    nx, ny, nz = dims
    row, col = lax.axis_index("row"), lax.axis_index("col")
    y, c = row // 2, row % 2
    x, z = col // nz, col % nz
    h = x % 2
    none = slots + 1
    half_k = nx * nz // 2
    half_x = nx // 2

    def wrap(v, n):
        return jnp.where(v >= n, v - n, v)

    xs = [x] + [wrap(x + d, nx) for d in range(1, nx)]
    yy = [y] + [wrap(y + d, ny) for d in range(1, ny)]
    zz = [z] + [wrap(z + d, nz) for d in range(1, nz)]

    def at(xv, yv, zv, cv):
        return (yv * 2 + cv, xv * nz + zv)

    partner = at(x, y, z, 1 - c)
    pair_y = jnp.where(h == 0, xs[1], xs[nx - 1])
    pair_z = jnp.where(h == 0, xs[nx - 1], xs[1])

    def remote(src, dst, ss, rs, device):
        return pltpu.make_async_remote_copy(src, dst, ss, rs, device_id=device, device_id_type=MESH)

    def loads(s):
        return (
            pltpu.make_async_copy(lhat.at[s], both.at[s, 0], in_sem.at[s]),
            pltpu.make_async_copy(ainv.at[s], both.at[s, 1], in_sem.at[s]),
        )

    fac_load = pltpu.make_async_copy(dinv.at[0], fac, in_sem.at[slots])
    ids_load = pltpu.make_async_copy(targets, ids, in_sem.at[slots + 1])
    ids_load.start()
    fac_load.start()
    for s in range(slots):
        for load in loads(s):
            load.start()

    barrier = pltpu.get_barrier_semaphore()
    peers = [partner, at(x, yy[1], z, c), at(x, yy[ny - 1], z, c), at(x, y, zz[1], c), at(x, y, zz[nz - 1], c)]
    for d in range(1, nx):
        peers += [at(xs[d], y, z, c), at(xs[d], y, z, 1 - c)]
    for peer in peers:
        pl.semaphore_signal(barrier, inc=1, device_id=peer, device_id_type=MESH)

    prod[none] = jnp.zeros(prod.shape[1:], jnp.float32)
    rx_u[none] = jnp.zeros(rx_u.shape[1:], jnp.float32)
    rx_d[none] = jnp.zeros(rx_d.shape[1:], jnp.float32)
    for i in range(2):
        rx_p[i, none] = jnp.zeros(rx_p.shape[2:], jnp.float32)

    def put(s, value, before):
        for i in range(2):
            part = value[:, i * LANES : (i + 1) * LANES].reshape(prod.shape[2:])
            prod[s, i] = part if before is None else prod[before, i] - part

    ids_load.wait()

    def table(k, carry):
        found = jnp.where(col == k, 0, none)
        for s in range(slots):
            found = jnp.where(ids[s] == k, s + 1, found)
        last_a[k] = found
        return carry

    lax.fori_loop(0, nx * nz, table, 0)
    fac_load.wait()
    put(0, transposed_product(fac[...], fac[...]), None)
    pl.semaphore_wait(barrier, len(peers))

    to_py = at(pair_y, y, z, 0)
    to_pz = at(pair_z, y, z, 1)
    tables = [
        remote(last_a, last_o.at[0], t_s, t_r.at[0], partner),
        remote(last_a, last_o.at[1 + c], t_s, t_r.at[1], to_py),
        remote(last_a, last_o.at[1 + c], t_s, t_r.at[1], to_pz),
    ]
    for copy in tables:
        copy.start()

    def exchanges(s):
        return (
            remote(prod.at[s, 0, :, 1 - h, 1], rx_p.at[c, s], xp_s, xp_r, to_py),
            remote(prod.at[s, 1, :, 1 - h, 1], rx_p.at[c, s], xp_s, xp_r, to_pz),
            remote(prod.at[s, :, :, 1 - c, 0], rx_u.at[s], xu_s, xu_r, partner),
            remote(prod.at[s, 1 - c, :, h, 1], rx_d.at[s], xd_s, xd_r, partner),
        )

    for s in range(slots):
        pltpu.make_async_copy(both.at[s], both.at[s], in_sem.at[s]).wait()
        value = transposed_product(both[s, 0], both[s, 1])
        before = jnp.where(ids[s] == col, 0, none)
        for e in range(s):
            before = jnp.where(ids[e] == ids[s], e + 1, before)
        put(s + 1, value, before)
        for copy in exchanges(s):
            copy.start()
    for copy in exchanges(slots):
        copy.start()

    def local_uy(k, yb):
        return prod[last_a[k], 0, yb, c, 0] + rx_u[last_o[0, k], 0, yb]

    def local_uz(k):
        return prod[last_a[k], 1, :, c, 0] + rx_u[last_o[0, k], 1]

    def local_py(k, yb):
        own = prod[last_a[k], 0, yb, h, 1] + rx_d[last_o[0, k], yb]
        return own + (rx_p[0, last_o[1, k], yb] + rx_p[1, last_o[2, k], yb])

    def local_pz(k):
        own = prod[last_a[k], 1, :, h, 1] + rx_d[last_o[0, k]]
        return own + (rx_p[0, last_o[1, k]] + rx_p[1, last_o[2, k]])

    unroll = 4 if half_k % 4 == 0 else 1

    def over_k(body):
        def some(i, carry):
            for j in range(unroll):
                body(i * unroll + j)
            return carry

        lax.fori_loop(0, half_k // unroll, some, 0)

    parts = {
        "uy": (st_uy, rc_uy, uys, uyr, local_uy, ny, yy),
        "uz": (st_uz, rc_uz, uzs, uzr, local_uz, nz, zz),
        "py": (st_py, rc_py, ps, pr, local_py, ny, yy),
        "pz": (st_pz, rc_pz, ps, pr, local_pz, nz, zz),
    }

    def place_of(which, way, half, hop):
        n = parts[which][5]
        hops = n // 2 if half == way else n // 2 - 1
        return hops, (0 if half == way else n // 2) + hop

    def message(which, way, m):
        st, rc, ss, rs, _, n, at_axis = parts[which]
        to = at_axis[1 if way == 0 else n - 1]
        device = at(x, to, z, c) if which[1] == "y" else at(x, y, to, c)
        return remote(st.at[way, m], rc.at[way, m], ss, rs.at[way, m], device)

    def terms(which, half, dest, dst):
        local = parts[which][4]
        if which[1] == "y":
            def body(k):
                dst[k] = local(half * half_k + k, dest)

            over_k(body)
        else:
            for i in range(half_x):
                dst[i] = local((half * half_x + i) * nz + dest)

    def flows(which, hop):
        for late in (0, 1):
            for way in (0, 1):
                half = way if late == 0 else 1 - way
                hops, m = place_of(which, way, half, hop)
                if hop < hops:
                    yield way, half, hops, m

    def prepare(which, hop):
        st, _, _, _, _, n, at_axis = parts[which]
        for way, half, hops, m in flows(which, hop):
            dest = at_axis[(hops - hop) % n if way == 0 else (n - hops + hop) % n]
            terms(which, half, dest, st.at[way, m])

    def go(whiches, hop):
        lists = [[(w, f) for f in flows(w, hop)] for w in whiches]
        for i in range(max(len(found) for found in lists)):
            for found in lists:
                if i >= len(found):
                    continue
                which, (way, half, hops, m) = found[i]
                st, rc = parts[which][0], parts[which][1]
                if hop > 0:
                    message(which, way, m - 1).wait_recv()
                    st[way, m] = st[way, m] + rc[way, m - 1]
                message(which, way, m).start()

    def finish(which, fin):
        _, rc, _, _, _, n, at_axis = parts[which]
        for half in (0, 1):
            for way in (0, 1):
                hops, m = place_of(which, way, half, 0)
                if hops == 0:
                    continue
                m = m + hops - 1
                message(which, way, m).wait_recv()
                fin[half] = fin[half] + rc[way, m]

    def prepare_final(which, fin):
        for half in (0, 1):
            terms(which, half, parts[which][6][0], fin.at[half])

    def for_core(first, second):
        pl.when(c == 0)(first)
        pl.when(c == 1)(second)

    rounds = max(ny, nz) // 2

    def p_round(hop):
        def run(which):
            def body():
                prepare(which, hop)
                go([which], hop)

            return body

        if hop < rounds:
            for_core(run("py"), run("pz"))

    used = pl.ds(0, slots + 1)

    def whole(ref, sem):
        return remote(ref, ref, sem, sem, partner)

    tables[0].wait_recv()
    whole(rx_u.at[used], xu_r).wait_recv()

    def u_round(hop):
        if hop < rounds:
            prepare("uy", hop)
            prepare("uz", hop)
            go(["uy", "uz"], hop)

    u_round(0)
    u_round(1)
    whole(last_o.at[pl.ds(1, 2)], t_r.at[1]).wait_recv()
    whole(rx_d.at[used], xd_r).wait_recv()
    whole(rx_p.at[:, used], xp_r).wait_recv()
    p_round(0)
    u_round(2)
    p_round(1)
    u_round(3)
    p_round(2)
    prepare_final("uy", fin_uy)
    prepare_final("uz", fin_uz)
    finish("uy", fin_uy)
    finish("uz", fin_uz)

    def far(d, n):
        return min(d, n - d)

    xz = sorted(((dx, dz) for dx in range(nx) for dz in range(nz)), key=lambda p: -far(p[0], nx) - far(p[1], nz))
    xy = sorted(((dx, dy) for dx in range(nx) for dy in range(ny)), key=lambda p: -far(p[0], nx) - far(p[1], ny))
    here_z = x * ny + y

    def src_y(fin, dx, dz):
        k = xs[dx] * nz + zz[dz]
        return fin.at[xs[dx] // half_x, k - (xs[dx] // half_x) * half_k]

    def src_z(fin, dx, dy):
        upper = xs[dx] // half_x
        return fin.at[upper, xs[dx] - upper * half_x, yy[dy]]

    def send_uy(dx, dz):
        return remote(
            src_y(fin_uy, dx, dz), r2_uy.at[col], fus.at[0], fuyr, at(xs[dx], y, zz[dz], c)
        )

    def send_uz(dx, dy):
        return remote(
            src_z(fin_uz, dx, dy), r2_uz.at[here_z], fus.at[1], fuzr, at(xs[dx], yy[dy], z, c)
        )

    def send_py(dx, dz):
        return remote(
            src_y(fin_py, dx, dz), r2_py.at[col], fps, fpyr, at(xs[dx], y, zz[dz], h)
        )

    def send_pz(dx, dy):
        return remote(
            src_z(fin_pz, dx, dy), r2_pz.at[here_z], fps, fpzr, at(xs[dx], yy[dy], z, h)
        )

    for i in range(max(len(xz), len(xy))):
        if i < len(xz) and xz[i] != (0, 0):
            send_uy(*xz[i]).start()
        if i < len(xy) and xy[i] != (0, 0):
            send_uz(*xy[i]).start()

    p_round(3)

    def p_final(which, fin, pairs, send, keep):
        def body():
            prepare_final(which, fin)
            finish(which, fin)
            for pair in pairs:
                if pair == (0, 0):
                    pl.when(h == c)(keep)
                    pl.when(h != c)(lambda: send(0, 0).start())
                else:
                    send(*pair).start()

        return body

    def keep_y():
        r2_py[col] = src_y(fin_py, 0, 0)[...]

    def keep_z():
        r2_pz[here_z] = src_z(fin_pz, 0, 0)[...]

    for_core(
        p_final("py", fin_py, xz, send_py, keep_y),
        p_final("pz", fin_pz, xy, send_pz, keep_z),
    )

    whole(last_o, t_s).wait_send()
    whole(rx_u.at[used], xu_s).wait_send()
    whole(rx_d.at[used], xd_s).wait_send()
    whole(rx_p.at[:, used], xp_s).wait_send()
    whole(st_uy, uys).wait_send()
    whole(st_uz, uzs).wait_send()
    for_core(lambda: whole(st_py, ps).wait_send(), lambda: whole(st_pz, ps).wait_send())

    def collect(r2, skip, first):
        total = first
        for k in range(r2.shape[0]):
            total = total + jnp.where(skip == k, 0.0, r2[k])
        return total

    n_y, n_z = nx * nz, nx * ny
    whole(r2_uy.at[pl.ds(0, n_y - 1)], fuyr).wait_recv()
    out[0, 0:SUB, 0:LANES] = collect(r2_uy, col, src_y(fin_uy, 0, 0)[...])
    whole(r2_uz.at[pl.ds(0, n_z - 1)], fuzr).wait_recv()
    out[0, 0:SUB, LANES:] = collect(r2_uz, here_z, src_z(fin_uz, 0, 0)[...])

    def collect_p(r2, sem, n, own_core):
        mine = (h == c) & (c == own_core)
        pl.when(mine)(lambda: whole(r2.at[pl.ds(0, half_x * n - 1)], sem).wait_recv())
        pl.when(jnp.logical_not(mine))(lambda: whole(r2.at[pl.ds(0, half_x * n)], sem).wait_recv())
        total = None
        for i in range(half_x):
            for d in range(n):
                value = r2[(2 * i + c) * n + d]
                total = value if total is None else total + value
        return total

    out[0, SUB:, 0:LANES] = collect_p(r2_py, fpyr, nz, 0)
    out[0, SUB:, LANES:] = collect_p(r2_pz, fpzr, ny, 1)

    whole(r2_uy.at[pl.ds(0, n_y - 1)], fus.at[0]).wait_send()
    whole(r2_uz.at[pl.ds(0, n_z - 1)], fus.at[1]).wait_send()

    def p_sent(n):
        pl.when(h == c)(lambda: whole(r2_py.at[pl.ds(0, n - 1)], fps).wait_send())
        pl.when(h != c)(lambda: whole(r2_py.at[pl.ds(0, n)], fps).wait_send())

    for_core(lambda: p_sent(n_y), lambda: p_sent(n_z))


def on_device(dims, lhat, ainv_anc, diag_inv, targets):
    nx, ny, nz = dims
    slots, height, width = lhat.shape
    f32 = jnp.float32
    dma = pltpu.SemaphoreType.DMA
    k_all, half_k, half_x = nx * nz, nx * nz // 2, nx // 2
    tile = (SUB, LANES)

    def vm(*lead):
        return pltpu.VMEM((*lead, *tile), f32)

    stages_y = [vm(2, ny - 1, half_k)]
    stages_z = [vm(2, nz - 1, half_x, ny)]
    scratch = [
        pltpu.VMEM((slots, 2, height, width), f32),
        pltpu.VMEM(diag_inv.shape[1:], f32),
        pltpu.SMEM((slots,), jnp.int32),
        vm(slots + 2, 2, ny, 2, 2),
        vm(slots + 2, 2, ny),
        vm(slots + 2, ny),
        vm(2, slots + 2, ny),
        pltpu.SMEM((k_all,), jnp.int32),
        pltpu.SMEM((3, k_all), jnp.int32),
        *(stages_y + stages_z) * 4,
        *[vm(2, half_k), vm(2, half_x, ny)] * 2,
        *[vm(k_all), vm(nx * ny)] * 2,
        dma((slots + 2,)),
        *[dma] * 6,
        dma,
        dma((2,)),
        dma,
        dma((2, ny - 1)),
        dma,
        dma((2, nz - 1)),
        dma,
        dma((2, max(ny, nz) - 1)),
        dma((2,)),
        *[dma] * 5,
    ]
    return pl.pallas_call(
        functools.partial(kernel, dims, slots),
        out_shape=jax.ShapeDtypeStruct(diag_inv.shape, f32),
        in_specs=[pl.BlockSpec(memory_space=pltpu.HBM)] * 4,
        out_specs=pl.BlockSpec(memory_space=pltpu.VMEM),
        scratch_shapes=scratch,
        compiler_params=pltpu.CompilerParams(
            collective_id=0, has_side_effects=True
        ),
        name="selected_blocks",
    )(lhat, ainv_anc, diag_inv, targets.reshape(slots))


def solution(mesh, nz=8):
    dims = (mesh.shape["col"] // nz, mesh.shape["row"] // 2, nz)
    placed = (
        P(("row", "col"), None, None),
        P(("row", "col"), None, None),
        P("col", "row", None),
        P(("row", "col"), None),
    )
    return jax.shard_map(
        functools.partial(on_device, dims), mesh=mesh, in_specs=placed, out_specs=P("col", "row", None), check_vma=False
    )
```

time: 125 us -> 49.6 us (0.40)
  waiting for transfers between devices: 59.4 us -> 0 us
  Pallas kernels: 0 us -> 48.1 us
  starting transfers between devices: 25.5 us -> 0 us
  blocking collectives: 25.2 us -> 0 us
  matrix products: 8.59 us -> 0 us
  local copies, waits for them, and re-layouts: 5.56 us -> 1.32 us
    all_to_all x3 -> x0, waiting for transfers between devices: 59.4 us -> none  [the longest x1 47.9 us: on_device(): lax.all_to_all(products, 'row', split_axis=1, concat_axis=0, tiled=True)]
    pallas_call x0 -> x1, Pallas kernels: none -> 48.1 us  [on_device(): pl.pallas_call(functools.partial(kernel, dims, slots), out_shape=jax.Shap...]
    all_to_all x3 -> x0, starting transfers between devices: 25.5 us -> none  [the longest x2 18.2 us: copy_for_each(): lax.all_to_all(jnp.broadcast_to(x[None], (length, *x.shape)), axis, 0, 0,...]
    all_to_all x1 -> x0, blocking collectives: 25.2 us -> none  [summed_on_arrival(): tiles = lax.all_to_all(in_blocks(x, dim, length), axis, 0, 0, tiled=True)]
    dot_general x3 -> x0, matrix products: 8.59 us -> none  [the longest x1 5.11 us: on_device(): jnp.einsum('shi,shj->sij', lhat, ainv_anc, precision=lax.Precision.HIGHEST)]
    neg x1 -> x0, local copies, waits for them, and re-layouts: 2.52 us -> none  [on_device(): -jnp.einsum('shi,shj->sij', lhat, ainv_anc, precision=lax.Precision.HIGHEST)]
    broadcast_in_dim x2 -> x0, local copies, waits for them, and re-layouts: 2.12 us -> none  [copy_for_each(): jnp.broadcast_to(x[None], (length, *x.shape))]
    unnamed x4 -> x1, local copies, waits for them, and re-layouts: 0.01 us -> 1.32 us
  transfers between devices with their start and end apart: 3 -> 0, of which waited for: 2 -> 0; matrix products, arithmetic and copies ran while one was open for 7% -> 0% of each run, Pallas kernels for 0% -> 0%
where the time goes in v2:
time: 49.6 us; the launch traced here: 49.4 us
  Pallas kernels  48.1 us (97%)
  local copies, waits for them, and re-layouts  1.32 us (3%)
    pallas_call x1, Pallas kernels, on_device(): pl.pallas_call(functools.partial(kernel, dims, slots), out_shape=jax.Shap...  48.1 us
    unnamed x1, local copies, waits for them, and re-layouts  1.32 us

profile of v2, /device:TPU:1, one launch (start us, length us, event | category | flops | bytes accessed | tf_op | source)
XLA Modules:
  0.0 49.4 jit_solution(14502440760035291692)
XLA Ops:
  0.0 48.1 %selected_blocks.1 = f32[1,16,256]{2,1,0:T(8,128)} custom-call(f32[8,256,256]{2,1,0:T(8,128)} %lhat.1, f32[8,256,256]{2,1,0:T(8,128)} %ainv.1, f32[1,16,256]{2,1,0:T(8,128)} %dinv.1, s32[8]{0:T(128)} %bitcast.1), custom_call_target="tpu_custom_call" | custom-call | tf_op jit(solution)/shard_map/selected_blocks/pallas_call | solution.py:432
  48.1 1.3 %copy.6 = f32[1,16,256]{2,1,0:T(8,128)} copy(f32[1,16,256]{2,1,0:T(8,128)} %selected_blocks.1) | data formatting | bytes 32768

commit v3 on v2

v3 whole, which is shorter than its diff:
```python
import functools

import jax
import jax.numpy as jnp
from jax import lax
from jax.experimental import pallas as pl
from jax.experimental.pallas import tpu as pltpu
from jax.sharding import PartitionSpec as P

MESH = pl.DeviceIdType.MESH
LANES = 128
SUB = 8
U, V = 1, 0


def split(x):
    hi = x.astype(jnp.bfloat16)
    lo = (x - hi.astype(jnp.float32)).astype(jnp.bfloat16)
    return hi, lo


def transposed_product(a, b):
    ah, al = split(a)
    bh, bl = split(b)
    left = jnp.concatenate([ah, ah, al], axis=0)
    right = jnp.concatenate([bh, bl, bh], axis=0)
    return lax.dot_general(left, right, (((0,), (0,)), ((), ())), preferred_element_type=jnp.float32)


def kernel(
    dims, slots,
    lhat, ainv, dinv, targets, out,
    both, fac, ids, prod, rx_u, rx_d, rx_p, last_a, last_o,
    st_uy, st_uz, st_py, st_pz, rc_uy, rc_uz, rc_py, rc_pz,
    fin_uy, fin_uz, fin_py, fin_pz, r2_uy, r2_uz, r2_py, r2_pz,
    in_sem, d_s, d_r, xp_s, xp_r, t_s, t_r,
    ys, yr, zs, zr, fs, fuyr, fuzr, fpyr, fpzr,
):
    nx, ny, nz = dims
    row, col = lax.axis_index("row"), lax.axis_index("col")
    y, c = row // 2, row % 2
    x, z = col // nz, col % nz
    h = x % 2
    none = slots + 1
    half_x = nx // 2

    def wrap(v, n):
        return jnp.where(v >= n, v - n, v)

    xs = [x] + [wrap(x + d, nx) for d in range(1, nx)]
    yy = [y] + [wrap(y + d, ny) for d in range(1, ny)]
    zz = [z] + [wrap(z + d, nz) for d in range(1, nz)]

    def at(xv, yv, zv, cv):
        return (yv * 2 + cv, xv * nz + zv)

    partner = at(x, y, z, 1 - c)
    pair_y = jnp.where(h == 0, xs[1], xs[nx - 1])
    pair_z = jnp.where(h == 0, xs[nx - 1], xs[1])

    def remote(src, dst, ss, rs, device):
        return pltpu.make_async_remote_copy(src, dst, ss, rs, device_id=device, device_id_type=MESH)

    def loads(s):
        return (
            pltpu.make_async_copy(lhat.at[s], both.at[s, 0], in_sem.at[s]),
            pltpu.make_async_copy(ainv.at[s], both.at[s, 1], in_sem.at[s]),
        )

    fac_load = pltpu.make_async_copy(dinv.at[0], fac, in_sem.at[slots])
    ids_load = pltpu.make_async_copy(targets, ids, in_sem.at[slots + 1])
    ids_load.start()
    fac_load.start()
    for s in range(slots):
        for load in loads(s):
            load.start()

    barrier = pltpu.get_barrier_semaphore()
    peers = [partner, at(x, yy[1], z, c), at(x, yy[ny - 1], z, c), at(x, y, zz[1], c), at(x, y, zz[nz - 1], c)]
    for d in range(1, nx):
        peers += [at(xs[d], y, z, c), at(xs[d], y, z, 1 - c)]
    if (nx, ny, nz) == (4, 8, 8):
        for d in (2, 6):
            peers += [at(x, yy[d], z, c), at(x, y, zz[d], c)]
    for peer in peers:
        pl.semaphore_signal(barrier, inc=1, device_id=peer, device_id_type=MESH)

    prod[none] = jnp.zeros(prod.shape[1:], jnp.float32)
    rx_u[none] = jnp.zeros(rx_u.shape[1:], jnp.float32)
    rx_d[none] = jnp.zeros(rx_d.shape[1:], jnp.float32)
    for i in range(2):
        for j in range(2):
            rx_p[i, j, none] = jnp.zeros(rx_p.shape[3:], jnp.float32)

    def put(s, value, before):
        for i in range(2):
            part = value[:, i * LANES : (i + 1) * LANES].reshape(prod.shape[2:])
            prod[s, i] = part if before is None else prod[before, i] - part

    ids_load.wait()

    def table(k, carry):
        found = jnp.where(col == k, 0, none)
        for s in range(slots):
            found = jnp.where(ids[s] == k, s + 1, found)
        last_a[k] = found
        return carry

    lax.fori_loop(0, nx * nz, table, 0)
    fac_load.wait()
    put(0, transposed_product(fac[...], fac[...]), None)
    pl.semaphore_wait(barrier, len(peers))

    to_py = at(pair_y, y, z, V)
    to_pz = at(pair_z, y, z, V)
    tables = [
        remote(last_a, last_o.at[0], t_s, t_r.at[0], partner),
        remote(last_a, last_o.at[1 + c], t_s, t_r.at[1], to_py),
        remote(last_a, last_o.at[3 + c], t_s, t_r.at[1], to_pz),
    ]
    for copy in tables:
        copy.start()

    def across(s):
        return (
            remote(prod.at[s, 0, :, 1 - h, 1], rx_p.at[0, c, s], xp_s, xp_r, to_py),
            remote(prod.at[s, 1, :, 1 - h, 1], rx_p.at[1, c, s], xp_s, xp_r, to_pz),
        )

    def exchange(s):
        for copy in across(s):
            copy.start()

        @pl.when(c == U)
        def _():
            remote(prod.at[s, :, :, h, 1], rx_d.at[s], d_s, d_r, partner).start()

        @pl.when(c == V)
        def _():
            remote(prod.at[s, :, :, :, 0], rx_u.at[s], d_s, d_r, partner).start()

    for s in range(slots):
        pltpu.make_async_copy(both.at[s], both.at[s], in_sem.at[s]).wait()
        value = transposed_product(both[s, 0], both[s, 1])
        before = jnp.where(ids[s] == col, 0, none)
        for e in range(s):
            before = jnp.where(ids[e] == ids[s], e + 1, before)
        put(s + 1, value, before)
        exchange(s)
    exchange(slots)

    def local_uy(k, yb):
        return prod[last_a[k], 0, yb, :, 0] + rx_u[last_o[0, k], 0, yb]

    def local_uz(k):
        return prod[last_a[k], 1, :, :, 0] + rx_u[last_o[0, k], 1]

    def local_py(k, yb):
        own = prod[last_a[k], 0, yb, h, 1] + rx_d[last_o[0, k], 0, yb]
        return own + (rx_p[0, 0, last_o[1, k], yb] + rx_p[0, 1, last_o[2, k], yb])

    def local_pz(k):
        own = prod[last_a[k], 1, :, h, 1] + rx_d[last_o[0, k], 1]
        return own + (rx_p[1, 0, last_o[3, k]] + rx_p[1, 1, last_o[4, k]])

    parts = {
        "uy": (st_uy, rc_uy, ys, yr, local_uy, ny, yy),
        "uz": (st_uz, rc_uz, zs, zr, local_uz, nz, zz),
        "py": (st_py, rc_py, ys, yr, local_py, ny, yy),
        "pz": (st_pz, rc_pz, zs, zr, local_pz, nz, zz),
    }

    def place_of(which, way, q, hop):
        n = parts[which][5]
        long = (q < half_x) == (way == 0)
        hops = n // 2 if long else n // 2 - 1
        base = (q % half_x) * hops + (0 if long else half_x * (n // 2))
        return hops, base + hop

    def message(which, way, m):
        st, rc, ss, rs, _, n, at_axis = parts[which]
        to = at_axis[1 if way == 0 else n - 1]
        device = at(x, to, z, c) if which[1] == "y" else at(x, y, to, c)
        return remote(st.at[way, m], rc.at[way, m], ss, rs.at[way, m], device)

    def terms(which, q, dest, dst):
        local = parts[which][4]
        if which[1] == "y":
            for i in range(nz):
                dst[i] = local(q * nz + i, dest)
        else:
            dst[...] = local(q * nz + dest)

    def flows(which, hop):
        for late in (0, 1):
            for j in range(half_x):
                for way in (0, 1):
                    q = (way if late == 0 else 1 - way) * half_x + j
                    hops, m = place_of(which, way, q, hop)
                    if hop < hops:
                        yield way, q, hops, m

    def own(which, hop, way, q, hops, m):
        st, _, _, _, _, n, at_axis = parts[which]
        dest = at_axis[(hops - hop) % n if way == 0 else (n - hops + hop) % n]
        terms(which, q, dest, st.at[way, m])

    def prepare(which, hop):
        for flow in flows(which, hop):
            own(which, hop, *flow)

    def go(whiches, hop):
        lists = [[(w, f) for f in flows(w, hop)] for w in whiches]
        for i in range(max(len(found) for found in lists)):
            for found in lists:
                if i >= len(found):
                    continue
                which, (way, q, hops, m) = found[i]
                st, rc = parts[which][0], parts[which][1]
                if hop == 0:
                    own(which, hop, way, q, hops, m)
                else:
                    message(which, way, m - 1).wait_recv()
                    st[way, m] = st[way, m] + rc[way, m - 1]
                message(which, way, m).start()

    def finish(which, fin):
        _, rc, _, _, _, n, at_axis = parts[which]
        for q in range(nx):
            for way in (0, 1):
                hops, m = place_of(which, way, q, 0)
                if hops == 0:
                    continue
                m = m + hops - 1
                message(which, way, m).wait_recv()
                fin[q] = fin[q] + rc[way, m]

    def prepare_final(which, fin):
        for q in range(nx):
            terms(which, q, parts[which][6][0], fin.at[q])

    def hop_message(which, way, m, steps):
        st, rc, ss, rs, _, n, at_axis = parts[which]
        to = at_axis[steps if way == 0 else n - steps]
        device = at(x, to, z, c) if which[1] == "y" else at(x, y, to, c)
        return remote(st.at[way, m], rc.at[way, m], ss, rs.at[way, m], device)

    def strides(pair, fins):
        def term(which, way, m, q, steps):
            n, at_axis = parts[which][5:]
            terms(which, q, at_axis[steps if way == 0 else n - steps], parts[which][0].at[way, m])

        everything = [(which, way) for which in pair for way in (0, 1)]
        for j in range(2):
            for which, way in everything:
                term(which, way, 4 + j, way * 2 + j, 4)
                hop_message(which, way, 4 + j, 2).start()
        for q in (0, 2, 1, 3):
            for which, way in everything:
                term(which, way, q, q, 3)
                hop_message(which, way, q, 1).start()
        for q in range(4):
            for which, way in everything:
                term(which, way, 6 + q, q, 1)
        for q in range(4):
            for which, way in everything:
                term(which, way, 10 + q, q, 2)
        for which, fin in zip(pair, fins):
            prepare_final(which, fin)
        for q in (0, 2, 1, 3):
            for which, way in everything:
                st, rc = parts[which][:2]
                value = st[way, 10 + q]
                if q // 2 == way:
                    hop_message(which, way, 4 + q % 2, 2).wait_recv()
                    value = value + rc[way, 4 + q % 2]
                hop_message(which, way, q, 1).wait_recv()
                st[way, 10 + q] = value + rc[way, q]
                hop_message(which, way, 10 + q, 2).start()
        for q in range(4):
            for which, way in everything:
                hop_message(which, way, 6 + q, 1).start()
        for m, steps in ((6, 1), (10, 2)):
            for q in (0, 2, 1, 3):
                for which, fin in zip(pair, fins):
                    for way in (0, 1):
                        hop_message(which, way, m + q, steps).wait_recv()
                        fin[q] = fin[q] + parts[which][1][way, m + q]

    used = pl.ds(0, slots + 1)

    def whole(ref, sem):
        return remote(ref, ref, sem, sem, partner)

    tables[0].wait_recv()

    def far(d, n):
        return min(d, n - d)

    xz = sorted(((dx, dz) for dx in range(nx) for dz in range(nz)), key=lambda p: -far(p[0], nx) - far(p[1], nz))
    xy = sorted(((dx, dy) for dx in range(nx) for dy in range(ny)), key=lambda p: -far(p[0], nx) - far(p[1], ny))
    here_z = x * ny + y

    def src_y(fin, dx, dz):
        return fin.at[xs[dx], zz[dz]]

    def src_z(fin, dx, dy):
        return fin.at[xs[dx], yy[dy]]

    n_y, n_z = nx * nz, nx * ny

    def send_u(dx, d, to):
        return (
            remote(src_y(fin_uy, dx, d).at[to], r2_uy.at[col], fs.at[0], fuyr, at(xs[dx], y, zz[d], to)),
            remote(src_z(fin_uz, dx, d).at[to], r2_uz.at[here_z], fs.at[1], fuzr, at(xs[dx], yy[d], z, to)),
        )

    def send_p(dx, d):
        return (
            remote(src_y(fin_py, dx, d), r2_py.at[col], fs.at[0], fpyr, at(xs[dx], y, zz[d], h)),
            remote(src_z(fin_pz, dx, d), r2_pz.at[here_z], fs.at[1], fpzr, at(xs[dx], yy[d], z, h)),
        )

    def chains(first, second, fin_first, fin_second):
        for hop in range(max(ny, nz) // 2):
            if hop > 0:
                prepare(first, hop)
                prepare(second, hop)
            go([first, second], hop)
        prepare_final(first, fin_first)
        prepare_final(second, fin_second)
        finish(first, fin_first)
        finish(second, fin_second)

    def each(body):
        for i in range(max(len(xz), len(xy))):
            for which, pairs in enumerate((xz, xy)):
                if i < len(pairs):
                    body(which, *pairs[i])

    @pl.when(c == U)
    def _():
        whole(rx_u.at[used], d_r).wait_recv()
        chains("uy", "uz", fin_uy, fin_uz)

        def send(which, dx, d):
            for to in (V, U):
                if (dx, d, to) != (0, 0, U):
                    send_u(dx, d, to)[which].start()

        each(send)
        r2_uy[col] = src_y(fin_uy, 0, 0)[U]
        r2_uz[here_z] = src_z(fin_uz, 0, 0)[U]
        whole(rx_d.at[used], d_s).wait_send()
        whole(st_uy, ys).wait_send()
        whole(st_uz, zs).wait_send()

    @pl.when(c == V)
    def _():
        whole(last_o.at[pl.ds(1, 4)], t_r.at[1]).wait_recv()
        whole(rx_d.at[used], d_r).wait_recv()
        whole(rx_p.at[:, :, used], xp_r).wait_recv()
        if (nx, ny, nz) == (4, 8, 8):
            strides(("py", "pz"), (fin_py, fin_pz))
        else:
            chains("py", "pz", fin_py, fin_pz)

        def send(which, dx, d):
            if (dx, d) != (0, 0):
                send_p(dx, d)[which].start()

        each(send)

        @pl.when(h != V)
        def _():
            for copy in send_p(0, 0):
                copy.start()

        @pl.when(h == V)
        def _():
            r2_py[col] = src_y(fin_py, 0, 0)[...]
            r2_pz[here_z] = src_z(fin_pz, 0, 0)[...]

        whole(rx_u.at[used], d_s).wait_send()
        whole(st_py, ys).wait_send()
        whole(st_pz, zs).wait_send()

    whole(last_o.at[pl.ds(0, 3)], t_s).wait_send()
    whole(rx_p.at[0, :, used], xp_s).wait_send()

    finals = ((r2_uy, n_y, fs.at[0]), (r2_uz, n_z, fs.at[1]))

    def take(r2, sem, count, kept):
        pl.when(kept)(lambda: whole(r2.at[pl.ds(0, count - 1)], sem).wait_recv())
        pl.when(jnp.logical_not(kept))(lambda: whole(r2.at[pl.ds(0, count)], sem).wait_recv())

    def summed(values):
        values = list(values)
        while len(values) > 1:
            values = [a + b for a, b in zip(values[::2], values[1::2])] + values[len(values) // 2 * 2 :]
        return values[0]

    take(r2_uy, fuyr, n_y, c == U)
    out[0, 0:SUB, 0:LANES] = summed(r2_uy[k] for k in range(n_y))
    take(r2_uz, fuzr, n_z, c == U)
    out[0, 0:SUB, LANES:] = summed(r2_uz[k] for k in range(n_z))
    mine = (c == V) & (h == V)
    take(r2_py, fpyr, n_y // 2, mine)
    out[0, SUB:, 0:LANES] = summed(r2_py[(2 * i + c) * nz + d] for i in range(half_x) for d in range(nz))
    take(r2_pz, fpzr, n_z // 2, mine)
    out[0, SUB:, LANES:] = summed(r2_pz[(2 * i + c) * ny + d] for i in range(half_x) for d in range(ny))

    @pl.when(c == U)
    def _():
        for r2, n, sem in finals:
            whole(r2, sem).wait_send()
            whole(r2.at[pl.ds(0, n - 1)], sem).wait_send()

    @pl.when(c == V)
    def _():
        for r2, n, sem in finals:
            whole(r2.at[pl.ds(0, n - 1)], sem).wait_send()
            pl.when(h != V)(lambda: whole(r2.at[0], sem).wait_send())


def on_device(dims, lhat, ainv_anc, diag_inv, targets):
    nx, ny, nz = dims
    slots, height, width = lhat.shape
    f32 = jnp.float32
    dma = pltpu.SemaphoreType.DMA
    k_all = nx * nz
    my, mz = nx // 2 * (ny - 1), nx // 2 * (nz - 1)
    tile = (SUB, LANES)

    def vm(*lead):
        return pltpu.VMEM((*lead, *tile), f32)

    scratch = [
        pltpu.VMEM((slots, 2, height, width), f32),
        pltpu.VMEM(diag_inv.shape[1:], f32),
        pltpu.SMEM((slots,), jnp.int32),
        vm(slots + 2, 2, ny, 2, 2),
        vm(slots + 2, 2, ny, 2),
        vm(slots + 2, 2, ny),
        vm(2, 2, slots + 2, ny),
        pltpu.SMEM((k_all,), jnp.int32),
        pltpu.SMEM((5, k_all), jnp.int32),
        *[vm(2, my, nz, 2), vm(2, mz, ny, 2), vm(2, my, nz), vm(2, mz, ny)] * 2,
        *[vm(nx, nz, 2), vm(nx, ny, 2), vm(nx, nz), vm(nx, ny)],
        *[vm(k_all), vm(nx * ny)] * 2,
        dma((slots + 2,)),
        *[dma] * 5,
        dma((2,)),
        dma,
        dma((2, my)),
        dma,
        dma((2, mz)),
        dma((2,)),
        *[dma] * 4,
    ]
    return pl.pallas_call(
        functools.partial(kernel, dims, slots),
        out_shape=jax.ShapeDtypeStruct(diag_inv.shape, f32),
        in_specs=[pl.BlockSpec(memory_space=pltpu.HBM)] * 4,
        out_specs=pl.BlockSpec(memory_space=pltpu.VMEM),
        scratch_shapes=scratch,
        compiler_params=pltpu.CompilerParams(
            collective_id=0, has_side_effects=True
        ),
        name="selected_blocks",
    )(lhat, ainv_anc, diag_inv, targets.reshape(slots))


def solution(mesh, nz=8):
    dims = (mesh.shape["col"] // nz, mesh.shape["row"] // 2, nz)
    placed = (
        P(("row", "col"), None, None),
        P(("row", "col"), None, None),
        P("col", "row", None),
        P(("row", "col"), None),
    )
    return jax.shard_map(
        functools.partial(on_device, dims), mesh=mesh, in_specs=placed, out_specs=P("col", "row", None), check_vma=False
    )
```

time: 49.6 us -> 49.3 us (level)
  no operation moved by 1% of the time
where the time goes in v3:
time: 49.3 us; the launch traced here: 49.1 us
  Pallas kernels  47.8 us (97%)
  local copies, waits for them, and re-layouts  1.32 us (3%)
    pallas_call x1, Pallas kernels, on_device(): pl.pallas_call(functools.partial(kernel, dims, slots), out_shape=jax.Shap...  47.8 us
    unnamed x1, local copies, waits for them, and re-layouts  1.32 us

profile of v3, /device:TPU:1, one launch (start us, length us, event | category | flops | bytes accessed | tf_op | source)
XLA Modules:
  0.0 49.1 jit_solution(15797482037505562652)
XLA Ops:
  0.0 47.8 %selected_blocks.1 = f32[1,16,256]{2,1,0:T(8,128)} custom-call(f32[8,256,256]{2,1,0:T(8,128)} %lhat.1, f32[8,256,256]{2,1,0:T(8,128)} %ainv.1, f32[1,16,256]{2,1,0:T(8,128)} %dinv.1, s32[8]{0:T(128)} %bitcast.1), custom_call_target="tpu_custom_call" | custom-call | tf_op jit(solution)/shard_map/selected_blocks/pallas_call | solution.py:461
  47.8 1.3 %copy.6 = f32[1,16,256]{2,1,0:T(8,128)} copy(f32[1,16,256]{2,1,0:T(8,128)} %selected_blocks.1) | data formatting | bytes 32768

commit v4 on v3

--- a/solution.py
+++ b/solution.py
@@ -10,7 +10,7 @@
 MESH = pl.DeviceIdType.MESH
 LANES = 128
 SUB = 8
-U, V = 1, 0
+U, V = 0, 1
 
 
 def split(x):
@@ -79,9 +79,6 @@
     peers = [partner, at(x, yy[1], z, c), at(x, yy[ny - 1], z, c), at(x, y, zz[1], c), at(x, y, zz[nz - 1], c)]
     for d in range(1, nx):
         peers += [at(xs[d], y, z, c), at(xs[d], y, z, 1 - c)]
-    if (nx, ny, nz) == (4, 8, 8):
-        for d in (2, 6):
-            peers += [at(x, yy[d], z, c), at(x, y, zz[d], c)]
     for peer in peers:
         pl.semaphore_signal(barrier, inc=1, device_id=peer, device_id_type=MESH)
 
@@ -128,9 +125,6 @@
         )
 
     def exchange(s):
-        for copy in across(s):
-            copy.start()
-
         @pl.when(c == U)
         def _():
             remote(prod.at[s, :, :, h, 1], rx_d.at[s], d_s, d_r, partner).start()
@@ -138,6 +132,9 @@
         @pl.when(c == V)
         def _():
             remote(prod.at[s, :, :, :, 0], rx_u.at[s], d_s, d_r, partner).start()
+
+        for copy in across(s):
+            copy.start()
 
     for s in range(slots):
         pltpu.make_async_copy(both.at[s], both.at[s], in_sem.at[s]).wait()
@@ -239,54 +236,6 @@
         for q in range(nx):
             terms(which, q, parts[which][6][0], fin.at[q])
 
-    def hop_message(which, way, m, steps):
-        st, rc, ss, rs, _, n, at_axis = parts[which]
-        to = at_axis[steps if way == 0 else n - steps]
-        device = at(x, to, z, c) if which[1] == "y" else at(x, y, to, c)
-        return remote(st.at[way, m], rc.at[way, m], ss, rs.at[way, m], device)
-
-    def strides(pair, fins):
-        def term(which, way, m, q, steps):
-            n, at_axis = parts[which][5:]
-            terms(which, q, at_axis[steps if way == 0 else n - steps], parts[which][0].at[way, m])
-
-        everything = [(which, way) for which in pair for way in (0, 1)]
-        for j in range(2):
-            for which, way in everything:
-                term(which, way, 4 + j, way * 2 + j, 4)
-                hop_message(which, way, 4 + j, 2).start()
-        for q in (0, 2, 1, 3):
-            for which, way in everything:
-                term(which, way, q, q, 3)
-                hop_message(which, way, q, 1).start()
-        for q in range(4):
-            for which, way in everything:
-                term(which, way, 6 + q, q, 1)
-        for q in range(4):
-            for which, way in everything:
-                term(which, way, 10 + q, q, 2)
-        for which, fin in zip(pair, fins):
-            prepare_final(which, fin)
-        for q in (0, 2, 1, 3):
-            for which, way in everything:
-                st, rc = parts[which][:2]
-                value = st[way, 10 + q]
-                if q // 2 == way:
-                    hop_message(which, way, 4 + q % 2, 2).wait_recv()
-                    value = value + rc[way, 4 + q % 2]
-                hop_message(which, way, q, 1).wait_recv()
-                st[way, 10 + q] = value + rc[way, q]
-                hop_message(which, way, 10 + q, 2).start()
-        for q in range(4):
-            for which, way in everything:
-                hop_message(which, way, 6 + q, 1).start()
-        for m, steps in ((6, 1), (10, 2)):
-            for q in (0, 2, 1, 3):
-                for which, fin in zip(pair, fins):
-                    for way in (0, 1):
-                        hop_message(which, way, m + q, steps).wait_recv()
-                        fin[q] = fin[q] + parts[which][1][way, m + q]
-
     used = pl.ds(0, slots + 1)
 
     def whole(ref, sem):
@@ -360,10 +309,7 @@
         whole(last_o.at[pl.ds(1, 4)], t_r.at[1]).wait_recv()
         whole(rx_d.at[used], d_r).wait_recv()
         whole(rx_p.at[:, :, used], xp_r).wait_recv()
-        if (nx, ny, nz) == (4, 8, 8):
-            strides(("py", "pz"), (fin_py, fin_pz))
-        else:
-            chains("py", "pz", fin_py, fin_pz)
+        chains("py", "pz", fin_py, fin_pz)
 
         def send(which, dx, d):
             if (dx, d) != (0, 0):

time: 49.3 us -> 47 us (0.953)
  Pallas kernels: 47.8 us -> 45.5 us
    pallas_call x1, Pallas kernels: 47.8 us -> 45.5 us  [on_device(): pl.pallas_call(functools.partial(kernel, dims, slots), out_shape=jax.Shap...]
where the time goes in v4:
time: 47 us; the launch traced here: 46.8 us
  Pallas kernels  45.5 us (97%)
  local copies, waits for them, and re-layouts  1.32 us (3%)
    pallas_call x1, Pallas kernels, on_device(): pl.pallas_call(functools.partial(kernel, dims, slots), out_shape=jax.Shap...  45.5 us
    unnamed x1, local copies, waits for them, and re-layouts  1.32 us

profile of v4, /device:TPU:1, one launch (start us, length us, event | category | flops | bytes accessed | tf_op | source)
XLA Modules:
  0.0 46.8 jit_solution(448990643376357250)
XLA Ops:
  0.0 45.5 %selected_blocks.1 = f32[1,16,256]{2,1,0:T(8,128)} custom-call(f32[8,256,256]{2,1,0:T(8,128)} %lhat.1, f32[8,256,256]{2,1,0:T(8,128)} %ainv.1, f32[1,16,256]{2,1,0:T(8,128)} %dinv.1, s32[8]{0:T(128)} %bitcast.1), custom_call_target="tpu_custom_call" | custom-call | tf_op jit(solution)/shard_map/selected_blocks/pallas_call | solution.py:407
  45.5 1.3 %copy.6 = f32[1,16,256]{2,1,0:T(8,128)} copy(f32[1,16,256]{2,1,0:T(8,128)} %selected_blocks.1) | data formatting | bytes 32768

commit v5 on v4

--- a/solution.py
+++ b/solution.py
@@ -272,12 +272,13 @@
 
     def chains(first, second, fin_first, fin_second):
         for hop in range(max(ny, nz) // 2):
-            if hop > 0:
-                prepare(first, hop)
-                prepare(second, hop)
             go([first, second], hop)
-        prepare_final(first, fin_first)
-        prepare_final(second, fin_second)
+            if hop == 0:
+                for later in range(1, max(ny, nz) // 2):
+                    prepare(first, later)
+                    prepare(second, later)
+                prepare_final(first, fin_first)
+                prepare_final(second, fin_second)
         finish(first, fin_first)
         finish(second, fin_second)
 
@@ -346,15 +347,15 @@
             values = [a + b for a, b in zip(values[::2], values[1::2])] + values[len(values) // 2 * 2 :]
         return values[0]
 
-    take(r2_uy, fuyr, n_y, c == U)
-    out[0, 0:SUB, 0:LANES] = summed(r2_uy[k] for k in range(n_y))
-    take(r2_uz, fuzr, n_z, c == U)
-    out[0, 0:SUB, LANES:] = summed(r2_uz[k] for k in range(n_z))
     mine = (c == V) & (h == V)
     take(r2_py, fpyr, n_y // 2, mine)
     out[0, SUB:, 0:LANES] = summed(r2_py[(2 * i + c) * nz + d] for i in range(half_x) for d in range(nz))
     take(r2_pz, fpzr, n_z // 2, mine)
     out[0, SUB:, LANES:] = summed(r2_pz[(2 * i + c) * ny + d] for i in range(half_x) for d in range(ny))
+    take(r2_uy, fuyr, n_y, c == U)
+    out[0, 0:SUB, 0:LANES] = summed(r2_uy[k] for k in range(n_y))
+    take(r2_uz, fuzr, n_z, c == U)
+    out[0, 0:SUB, LANES:] = summed(r2_uz[k] for k in range(n_z))
 
     @pl.when(c == U)
     def _():

time: 47 us -> 47.2 us (level)
  no operation moved by 1% of the time
where the time goes in v5:
time: 47.2 us; the launch traced here: 47 us
  Pallas kernels  45.6 us (97%)
  local copies, waits for them, and re-layouts  1.32 us (3%)
    pallas_call x1, Pallas kernels, on_device(): pl.pallas_call(functools.partial(kernel, dims, slots), out_shape=jax.Shap...  45.6 us
    unnamed x1, local copies, waits for them, and re-layouts  1.32 us

profile of v5, /device:TPU:1, one launch (start us, length us, event | category | flops | bytes accessed | tf_op | source)
XLA Modules:
  0.0 47.0 jit_solution(11170023244806958372)
XLA Ops:
  0.0 45.6 %selected_blocks.1 = f32[1,16,256]{2,1,0:T(8,128)} custom-call(f32[8,256,256]{2,1,0:T(8,128)} %lhat.1, f32[8,256,256]{2,1,0:T(8,128)} %ainv.1, f32[1,16,256]{2,1,0:T(8,128)} %dinv.1, s32[8]{0:T(128)} %bitcast.1), custom_call_target="tpu_custom_call" | custom-call | tf_op jit(solution)/shard_map/selected_blocks/pallas_call | solution.py:408
  45.6 1.3 %copy.6 = f32[1,16,256]{2,1,0:T(8,128)} copy(f32[1,16,256]{2,1,0:T(8,128)} %selected_blocks.1) | data formatting | bytes 32768
